TPU v7x, 32 devices: a whole 2x2x4 slice. The times are simulated.
32 devices in a mesh: col: 8 (over z, x), bin: 4 (over y, core).
Axes of the slice: x: 2, y: 2, z: 4, core: 2. Of those that a mesh axis runs over, the one named last changes fastest.
Arguments:
- slope: float32 [131072], P('bin'), may hold values from -6 to 6
- curvature: float32 [131072], P('bin'), may hold values from -6 to 0
- target_mean: float32 [131072], P('bin'), may hold values from 0.15 to 0.85
- target_var: float32 [131072], P('bin'), may hold values from 0.06 to 0.12
- table: float32 [64, 512], P(None, 'col'), may hold values from -6 to 6
Outputs:
- species_mean: float32 [64, 131072], P('col')
- final_slope: float32 [131072], replicated
All inputs are finite; a program needn't handle non-finite values.
Results may differ from a plain program's by a relative error of at most 0.0001.
Values sent between devices are 32-bit elements; how exact they have to be, the bound alone decides.
A program may use at most 64 MiB of HBM per device.

v0:
```python
import functools
import math
import jax
import jax.numpy as jnp
from jax import lax
from jax.experimental import pallas as pl
from jax.experimental.pallas import tpu as pltpu
from jax.sharding import PartitionSpec as P

ITERS = 3
LANES = 128
LOG2E = math.log2(math.e)
MESH = pl.DeviceIdType.MESH
UNROLL = 16
GROUP = 4
PARTS = 4


def kernel(
    cols, bins, total_pts, rows,
    slope_hbm, curve_hbm, mean_hbm, var_hbm, placed_ref,
    out_ref, lam_ref,
    own, curve, tab, lhs, points, stage, species,
    isem, tsend, trecv, ksend, krecv, asend, arecv, bsend, brecv, lsend, lrecv,
    msend, mrecv, ysend, yrecv, psend, precv, osem,
):
    col = lax.axis_index("col")
    me = lax.axis_index("bin")
    core = lax.rem(me, 2)
    partner = me + 1 - 2 * core
    chips = bins // 2
    groups = cols // GROUP
    member = lax.rem(col, GROUP)
    group = col // GROUP
    sub = own.shape[1]
    width = sub * LANES
    part = width // PARTS
    part_rows = sub // PARTS
    pad = placed_ref.shape[1]

    def other_chip(i):
        return lax.rem(me + 2 * i, bins)

    def peer(u, d):
        return lax.rem(group + u, groups) * GROUP + lax.rem(member + d, GROUP)

    def remote(src, dst, send, recv, c, b):
        return pltpu.make_async_remote_copy(
            src_ref=src, dst_ref=dst, send_sem=send, recv_sem=recv,
            device_id=(c, b), device_id_type=MESH,
        )

    barrier = pltpu.get_barrier_semaphore()

    @pl.loop(1, cols)
    def _(i):
        pl.semaphore_signal(barrier, inc=1, device_id=(lax.rem(col + i, cols), me), device_id_type=MESH)

    for i in range(1, chips):
        @pl.loop(0, groups)
        def _(u):
            pl.semaphore_signal(barrier, inc=1, device_id=(peer(u, 0), other_chip(i)), device_id_type=MESH)

    pl.semaphore_signal(barrier, inc=1, device_id=(col, partner), device_id_type=MESH)

    loads = [
        pltpu.make_async_copy(a.at[col], own.at[n], isem.at[n])
        for n, a in enumerate((slope_hbm, mean_hbm, var_hbm))
    ]
    loads.append(pltpu.make_async_copy(curve_hbm, curve.at[me], isem.at[3]))
    for load in loads:
        load.start()
    tab[col] = placed_ref[pl.ds(group * GROUP, GROUP)]
    points[...] = (lax.broadcasted_iota(jnp.int32, points.shape, 0).astype(jnp.float32) + 0.5) * (1.0 / total_pts)
    for load in loads:
        load.wait()

    curve2 = curve[me, col] * LOG2E
    target = own[1]
    var = own[2]
    lam = own[0]

    h = 1.0 / total_pts
    bend = jnp.exp2(curve2 * (2.0 * h * h))

    def newton(lam):
        lam2 = lam * LOG2E

        def body(g, carry):
            total, mom = carry
            c = ((g * UNROLL).astype(jnp.float32) + 0.5) * h
            e = jnp.exp2(c * (lam2 + curve2 * c))
            ratio = jnp.exp2(h * (lam2 + curve2 * (2.0 * c + h)))
            run = e
            runs = e
            for i in range(1, UNROLL):
                e = e * ratio
                if i < UNROLL - 1:
                    ratio = ratio * bend
                run = run + e
                runs = runs + run
            return total + run, mom + (c * run + h * (UNROLL * run - runs))

        zero = jnp.zeros_like(lam)
        total, mom = lax.fori_loop(0, total_pts // UNROLL, body, (zero, zero))
        return lam + (target - mom / total) / var

    lam = newton(lam)
    pl.semaphore_wait(barrier, cols - 1 + (chips - 1) * groups + 1)

    def table_copy(i):
        to = lax.rem(col + i, cols)
        return remote(placed_ref.at[pl.ds(to // GROUP * GROUP, GROUP)], tab.at[col], tsend.at[i], trecv.at[col], to, me)

    def table_arrival(i):
        src = lax.rem(col + i, cols)
        return remote(tab.at[src], tab.at[src], tsend.at[i], trecv.at[src], src, me)

    def curve_copy(i, u):
        j = peer(u, 0)
        to = other_chip(i)
        return remote(curve.at[me, j], curve.at[me, j], ksend.at[i, u], krecv.at[me // 2, j], col, to)

    def curve_arrival(i, u):
        j = peer(u, 0)
        b = other_chip(i)
        return remote(curve.at[b, j], curve.at[b, j], ksend.at[i, u], krecv.at[b // 2, j], col, b)

    @pl.loop(1, cols)
    def _(i):
        table_copy(i).start()

    for i in range(1, chips):
        @pl.loop(0, groups)
        def _(u):
            curve_copy(i, u).start()

    for step in range(1, ITERS):
        lam = newton(lam)
    lam_ref[me, col] = lam

    def first_copy(i, u):
        return remote(lam_ref.at[me, col], lam_ref.at[me, col], asend.at[i, u], arecv.at[me // 2, col], peer(u, 0), other_chip(i))

    def first_arrival(i, u):
        j = peer(u, 0)
        b = other_chip(i)
        return remote(lam_ref.at[b, j], lam_ref.at[b, j], asend.at[i, u], arecv.at[b // 2, j], j, b)

    @pl.loop(1, groups)
    def _(u):
        first_copy(0, u).start()

    for i in range(1, chips):
        @pl.loop(0, groups)
        def _(u):
            first_copy(i, u).start()

    @pl.loop(1, cols)
    def _(i):
        table_arrival(i).wait_recv()

    full = jnp.concatenate(
        [jnp.concatenate([tab[t, n] for n in range(GROUP)], axis=0) for t in range(cols)], axis=1
    )
    high = full.astype(jnp.bfloat16).astype(jnp.float32)
    ones = jnp.ones((16, total_pts), jnp.float32)
    lhs[...] = jnp.concatenate([high, full - high, ones], axis=0).astype(jnp.bfloat16)

    span = GROUP * pad

    def lanes(q):
        return pl.ds(pl.multiple_of(q * part, LANES), part)

    def compute(item, b, j, q):
        @pl.loop(0, part_rows // 2)
        def _(t):
            highs, lows = [], []
            for n in range(2):
                r = q * part_rows + t * 2 + n
                lam_t = lam_ref[b, j, pl.ds(r, 1)] * LOG2E
                cur_t = curve[b, j, pl.ds(r, 1)] * LOG2E
                c = points[...]
                e = jnp.exp2(c * (lam_t + cur_t * c))
                e_hi = e.astype(jnp.bfloat16)
                highs.append(e_hi)
                lows.append((e - e_hi.astype(jnp.float32)).astype(jnp.bfloat16))
            acc = jnp.dot(lhs[...], jnp.concatenate(highs, axis=1), preferred_element_type=jnp.float32)
            acc = acc + jnp.dot(lhs[...], jnp.concatenate(lows, axis=1), preferred_element_type=jnp.float32)
            value = (acc[:span] + acc[span:2 * span]) / acc[2 * span:2 * span + 1]
            at = pl.ds(pl.multiple_of(t * 2 * LANES, 2 * LANES), 2 * LANES)
            for n in range(GROUP):
                stage[item, n, :, at] = value[n * pad:n * pad + rows]
            into = pl.ds(pl.multiple_of(q * part + t * 2 * LANES, 2 * LANES), 2 * LANES)
            species[b, j, :, into] = stage[item, member, :, at]

    def member_copy(item, d, b, j, q):
        to = lax.rem(member + d, GROUP)
        return remote(stage.at[item, to], species.at[b, j, :, lanes(q)], msend.at[item, d], mrecv.at[b // 2, j, q], group * GROUP + to, me)

    def member_arrival(b, j, q):
        return remote(species.at[b, j, :, lanes(q)], species.at[b, j, :, lanes(q)], msend.at[0, 0], mrecv.at[b // 2, j, q], lax.rem(col + 1, cols), me)

    def y_copy(i, j, q):
        at = species.at[me, j, :, lanes(q)]
        return remote(at, at, ysend.at[i, j, q], yrecv.at[me // 2, j, q], col, other_chip(i))

    def y_arrival(i, j, q):
        b = other_chip(i)
        at = species.at[b, j, :, lanes(q)]
        return remote(at, at, ysend.at[i, j, q], yrecv.at[b // 2, j, q], col, b)

    def pair_copy(b, j, q):
        at = species.at[b, j, :, lanes(q)]
        return remote(at, at, psend.at[b // 2, j], precv.at[b // 2, j], col, partner)

    def pair_chunk(b, j):
        at = species.at[b, j]
        return remote(at, at, psend.at[b // 2, j], precv.at[b // 2, j], col, partner)

    def write_part(b, j, q):
        start = pl.multiple_of((b * cols + j) * width + q * part, LANES)
        return pltpu.make_async_copy(species.at[b, j, :, lanes(q)], out_ref.at[:, pl.ds(start, part)], osem.at[b, j])

    def write_chunk(b, j):
        start = pl.multiple_of((b * cols + j) * width, LANES)
        return pltpu.make_async_copy(species.at[b, j], out_ref.at[:, pl.ds(start, width)], osem.at[b, j])

    def hand_on(b, j, q):
        pair_copy(b, j, q).start()
        write_part(b, j, q).start()

    singles = groups * (PARTS - 1)

    def single(s):
        return s // (PARTS - 1), 1 + lax.rem(s, PARTS - 1)

    def single_arrivals(s):
        u, q = single(s)
        for d in range(1, GROUP):
            j = peer(u, d)
            member_arrival(me, j, q).wait_recv()
            for i in range(1, chips):
                y_copy(i, j, q).start()
            hand_on(me, j, q)

    @pl.loop(0, singles)
    def _(s):
        u, q = single(s)
        j = peer(u, 0)

        @pl.when(jnp.logical_and(q == 1, u > 0))
        def _():
            first_arrival(0, u).wait_recv()

        compute(s, me, j, q)
        for i in range(1, chips):
            y_copy(i, j, q).start()
        for d in range(1, GROUP):
            member_copy(s, d, me, j, q).start()
        hand_on(me, j, q)

        @pl.when(s > 1)
        def _():
            single_arrivals(s - 2)

    for i in range(1, chips):
        @pl.loop(0, groups)
        def _(u):
            first_arrival(i, u).wait_recv()
            curve_arrival(i, u).wait_recv()

    doubles = groups * chips

    @pl.loop(0, doubles)
    def _(s):
        u = s // chips
        b = lax.rem(me + 2 * lax.rem(s, chips), bins)
        j = peer(u, 0)
        compute(singles + s, b, j, 0)
        for d in range(1, GROUP):
            member_copy(singles + s, d, b, j, 0).start()
        hand_on(b, j, 0)

        @pl.when(s < 2)
        def _():
            single_arrivals(singles - 2 + s)

    def second_copy(d, b, j):
        to = lax.rem(member + d, GROUP)
        return remote(lam_ref.at[b, j], lam_ref.at[b, j], bsend.at[b // 2, j // GROUP, d], brecv.at[b // 2, j], group * GROUP + to, me)

    @pl.loop(0, doubles)
    def _(s):
        b = lax.rem(me + 2 * lax.rem(s, chips), bins)
        for d in range(1, GROUP):
            second_copy(d, b, peer(s // chips, 0)).start()

    @pl.loop(0, doubles)
    def _(s):
        b = lax.rem(me + 2 * lax.rem(s, chips), bins)
        for d in range(1, GROUP):
            j = peer(s // chips, d)
            member_arrival(b, j, 0).wait_recv()
            hand_on(b, j, 0)

    @pl.loop(0, singles)
    def _(s):
        u, q = single(s)
        for d in range(GROUP):
            for i in range(1, chips):
                y_arrival(i, peer(u, d), q).wait_recv()
                hand_on(other_chip(i), peer(u, d), q)

    def lam_pair(b):
        return remote(lam_ref.at[b], lam_ref.at[b], lsend.at[b // 2], lrecv.at[b // 2], col, partner)

    for i in range(chips):
        b = other_chip(i)

        @pl.loop(0, groups)
        def _(u):
            for d in range(1, GROUP):
                second_copy(d, b, peer(u, d)).wait_recv()

        lam_pair(b).start()

    @pl.loop(0, cols)
    def _(j):
        for i in range(chips):
            b = other_chip(i)
            theirs = lax.rem(partner + 2 * i, bins)
            pair_chunk(theirs, j).wait_recv()
            write_chunk(theirs, j).start()

    for i in range(chips):
        lam_pair(other_chip(i)).wait()

    @pl.loop(0, cols)
    def _(j):
        for b in range(bins):
            write_chunk(b, j).wait()
        for i in range(chips):
            pair_chunk(other_chip(i), j).wait_send()
        for i in range(1, chips):
            for q in range(1, PARTS):
                y_copy(i, j, q).wait_send()

    @pl.loop(0, singles + doubles)
    def _(item):
        for d in range(1, GROUP):
            member_copy(item, d, me, col, 0).wait_send()

    @pl.loop(0, doubles)
    def _(s):
        b = lax.rem(me + 2 * lax.rem(s, chips), bins)
        for d in range(1, GROUP):
            second_copy(d, b, peer(s // chips, 0)).wait_send()

    @pl.loop(1, groups)
    def _(u):
        first_copy(0, u).wait_send()

    for i in range(1, chips):
        @pl.loop(0, groups)
        def _(u):
            first_copy(i, u).wait_send()
            curve_copy(i, u).wait_send()

    @pl.loop(1, cols)
    def _(i):
        table_copy(i).wait_send()


def per_device(slope, curvature, target_mean, target_var, table):
    cols = lax.axis_size("col")
    bins = lax.axis_size("bin")
    all_species, pts = table.shape
    rows = all_species // cols
    pad = rows
    total_pts = pts * cols
    per_shard = slope.shape[0]
    sub = per_shard // cols // LANES
    width = sub * LANES
    chips = bins // 2
    groups = cols // GROUP
    items = groups * (PARTS - 1 + chips)

    def blocks(a):
        return a.reshape(cols, sub, LANES)

    placed = table.reshape(cols, rows, pts)
    vmem = pl.BlockSpec(memory_space=pltpu.VMEM)
    hbm = pl.BlockSpec(memory_space=pltpu.HBM)
    dma = pltpu.SemaphoreType.DMA
    species_mean, lam = pl.pallas_call(
        functools.partial(kernel, cols, bins, total_pts, rows),
        out_shape=(
            jax.ShapeDtypeStruct((rows, per_shard * bins), jnp.float32),
            jax.ShapeDtypeStruct((bins, cols, sub, LANES), jnp.float32),
        ),
        in_specs=[hbm] * 4 + [vmem],
        out_specs=(pl.BlockSpec(memory_space=pl.ANY), vmem),
        scratch_shapes=[
            pltpu.VMEM((3, sub, LANES), jnp.float32),
            pltpu.VMEM((bins, cols, sub, LANES), jnp.float32),
            pltpu.VMEM((cols, GROUP, pad, pts), jnp.float32),
            pltpu.VMEM((2 * GROUP * pad + 16, total_pts), jnp.bfloat16),
            pltpu.VMEM((total_pts, LANES), jnp.float32),
            pltpu.VMEM((items, GROUP, rows, width // PARTS), jnp.float32),
            pltpu.VMEM((bins, cols, rows, width), jnp.float32),
            dma((4,)),
            dma((cols,)), dma((cols,)),
            dma((chips, groups)), dma((chips, cols)),
            dma((chips, groups)), dma((chips, cols)),
            dma((chips, groups, GROUP)), dma((chips, cols)),
            dma((chips,)), dma((chips,)),
            dma((items, GROUP)), dma((chips, cols, PARTS)),
            dma((chips, cols, PARTS)), dma((chips, cols, PARTS)),
            dma((chips, cols)), dma((chips, cols)),
            dma((bins, cols)),
        ],
        compiler_params=pltpu.CompilerParams(collective_id=0, has_side_effects=True, vmem_limit_bytes=40 << 20),
    )(*[
        pltpu.with_memory_space_constraint(a, pltpu.HBM)
        for a in (blocks(slope), blocks(curvature), blocks(target_mean), blocks(target_var))
    ], placed)
    return species_mean, lam.reshape(-1)


def solution(mesh):
    placed = (P("bin"), P("bin"), P("bin"), P("bin"), P(None, "col"))
    return jax.shard_map(
        per_device, mesh=mesh, in_specs=placed, out_specs=(P("col", None), P()), check_vma=False
    )
```

profile of v0, /device:TPU:0, one launch (start us, length us, event | category | flops | bytes accessed | tf_op | source)
XLA Modules:
  0.0 43.5 jit_solution(12136822282123955286)
XLA Ops:
  0.6 0.0 copy-start
  0.6 0.7 %copy-done = f32[64,64]{1,0:T(8,128)S(1)} copy-done((f32[64,64]{1,0:T(8,128)S(1)}, f32[64,64]{1,0:T(8,128)}, u32[]{:S(2)}) %copy-start) | copy-done | bytes 16408
  1.4 39.2 %shard_map.68 = (f32[8,131072]{1,0:T(8,128)S(1)}, f32[4,8,32,128]{3,2,1,0:T(8,128)S(1)}) custom-call(f32[8,32,128]{2,1,0:T(8,128)} %bitcast.8, f32[8,32,128]{2,1,0:T(8,128)} %bitcast.9, f32[8,32,128]{2,1,0:T(8,128)} %bitcast.10, f32[8,32,128]{2,1,0:T(8,128)} %bitcast.11, f32[8,8,64]{2,1,0:T(8,128)S(1)} %bitcast.7), custom_call_target="tpu_custom_call" | custom-call | tf_op jit(solution)/shard_map/pallas_call | solution.py:396
  40.6 2.0 %copy.9 = f32[8,131072]{1,0:T(8,128)} copy(f32[8,131072]{1,0:T(8,128)S(1)} %get-tuple-element.8) | data formatting | bytes 8388608
  42.7 0.8 %copy.10 = f32[131072]{0:T(1024)} copy(f32[131072]{0:T(1024)S(1)} %bitcast.6) | data formatting | bytes 1048576
Async XLA Ops:
  0.6 0.8 %copy-start = (f32[64,64]{1,0:T(8,128)S(1)}, f32[64,64]{1,0:T(8,128)}, u32[]{:S(2)}) copy-start(f32[64,64]{1,0:T(8,128)} %param.9) | copy-start | bytes 49156
where the time goes:
time: 43.7 us; the launch traced here: 43.5 us
  Pallas kernels  39.2 us (90%)
  local copies, waits for them, and re-layouts  3.59 us (8%)
  between operations  0.65 us (1%)
    pallas_call x1, Pallas kernels, per_device(): pl.pallas_call(functools.partial(kernel, cols, bins, total_pts, rows), ou...  39.2 us
    unnamed x4, local copies, waits for them, and re-layouts  3.59 us

commit v1 on v0

v1 whole, which is shorter than its diff:
```python
import functools
import math
import jax
import jax.numpy as jnp
from jax import lax
from jax.experimental import pallas as pl
from jax.experimental.pallas import tpu as pltpu
from jax.sharding import PartitionSpec as P

ITERS = 3
LANES = 128
LOG2E = math.log2(math.e)
MESH = pl.DeviceIdType.MESH
UNROLL = 32
STRIDE = 32
GROUP = 4
PARTS = 4
SINGLE = 2


def kernel(
    cols, bins, total_pts, rows,
    slope_hbm, curve_hbm, mean_hbm, var_hbm, placed_hbm,
    species, lam_ref,
    own, curve, placed, tab, lhs, lhs_own, consts, stage,
    isem, far, tsend, trecv, ksend, krecv, asend, arecv, bsend, brecv, rsend, rrecv,
    lsend, lrecv, msend, mrecv, ysend, yrecv, psend, precv,
):
    col = lax.axis_index("col")
    me = lax.axis_index("bin")
    core = lax.rem(me, 2)
    partner = me + 1 - 2 * core
    chips = bins // 2
    groups = cols // GROUP
    member = lax.rem(col, GROUP)
    group = col // GROUP
    sub = own.shape[1]
    width = sub * LANES
    part = width // PARTS
    part_rows = sub // PARTS
    singles = groups * SINGLE

    def other_chip(i):
        return lax.rem(me + 2 * i, bins)

    def peer(u, d):
        return lax.rem(group + u, groups) * GROUP + lax.rem(member + d, GROUP)

    def remote(src, dst, send, recv, c, b):
        return pltpu.make_async_remote_copy(
            src_ref=src, dst_ref=dst, send_sem=send, recv_sem=recv,
            device_id=(c, b), device_id_type=MESH,
        )

    def total_of(ref, send, recv):
        return remote(ref, ref, send, recv, col, partner)

    loads = [
        pltpu.make_async_copy(a.at[col], own.at[n], isem.at[n])
        for n, a in enumerate((slope_hbm, mean_hbm, var_hbm))
    ]
    loads.append(pltpu.make_async_copy(curve_hbm, curve.at[me], isem.at[3]))
    load_table = pltpu.make_async_copy(placed_hbm, placed, isem.at[4])
    load_table.start()
    for load in loads:
        load.start()

    def greet(sem, c, b):
        pl.semaphore_signal(sem, inc=1, device_id=(c, b), device_id_type=MESH)

    barrier = pltpu.get_barrier_semaphore()
    greet(barrier, col, partner)
    for d in range(1, GROUP):
        greet(barrier, peer(0, d), me)
    for i in range(1, chips):
        greet(barrier, col, other_chip(i))

    def greet_group(sem, g):
        for d in range(GROUP):
            greet(sem, g * GROUP + d, me)
        for i in range(1, chips):
            greet(sem, g * GROUP + member, other_chip(i))

    @pl.loop(group + 1, groups)
    def _(g):
        greet_group(barrier, g)

    each = GROUP + chips - 1
    h = 1.0 / total_pts
    wide = STRIDE * h
    first = (lax.broadcasted_iota(jnp.int32, consts.shape[1:], 0).astype(jnp.float32) + 0.5) * h
    consts[0] = first
    consts[1] = wide * (2.0 * first + wide)

    def table_copy(to):
        return remote(placed.at[pl.ds(to // GROUP * GROUP, GROUP)], tab.at[col], tsend.at[0], trecv.at[0], to, me)

    def curve_copy(i):
        at = curve.at[me, :, pl.ds(0, 2 * part_rows)]
        return remote(at, at, ksend.at[0], krecv.at[0], col, other_chip(i))

    def enter():
        pl.semaphore_wait(barrier, (group + 1) * each)

        @pl.loop(0, group)
        def _(g):
            greet_group(far, g)

        load_table.wait()

        @pl.loop(0, group)
        def _(g):
            for d in range(GROUP):
                table_copy(g * GROUP + d).start()

        for d in range(1, GROUP):
            table_copy(peer(0, d)).start()
        tab[col] = placed[pl.ds(group * GROUP, GROUP)]

    for load in loads:
        load.wait()

    curve2 = curve[me, col] * LOG2E
    target = own[1]
    var = own[2]
    lam = own[0]
    bend = jnp.exp2(curve2 * (2.0 * h * h))

    def newton(lam):
        lam2 = lam * LOG2E

        def begin(g):
            c = ((g * UNROLL).astype(jnp.float32) + 0.5) * h
            return jnp.exp2(c * (lam2 + curve2 * c)), jnp.exp2(h * (lam2 + curve2 * (2.0 * c + h)))

        def body(g, carry):
            total, mom, e, ratio = carry
            later = begin(g + 1)
            c = ((g * UNROLL).astype(jnp.float32) + 0.5) * h
            run = e
            runs = e
            for i in range(1, UNROLL):
                e = e * ratio
                if i < UNROLL - 1:
                    ratio = ratio * bend
                run = run + e
                runs = runs + run
            return total + run, mom + (c * run + h * (UNROLL * run - runs)), *later

        zero = jnp.zeros_like(lam)
        total, mom, _, _ = lax.fori_loop(0, total_pts // UNROLL, body, (zero, zero, *begin(jnp.int32(0))))
        return lam + (target - mom / total) / var

    @pl.when(group == groups - 1)
    def _():
        enter()

    lam = newton(lam)

    @pl.when(group < groups - 1)
    def _():
        enter()

    for i in range(1, chips):
        curve_copy(i).start()

    for step in range(1, ITERS):
        lam = newton(lam)
    lam_ref[me, col] = lam

    @pl.when(group < groups - 1)
    def _():
        pl.semaphore_wait(far, (groups - 1 - group) * each)

        @pl.loop(group + 1, groups)
        def _(g):
            for d in range(GROUP):
                table_copy(g * GROUP + d).start()

    def first_copy(i, u):
        at = lam_ref.at[me, col]
        return remote(at, at, asend.at[0], arecv.at[(chips - i) % chips, lax.rem(groups - u, groups)], peer(u, 0), other_chip(i))

    def first_arrival(i, u):
        b, j = other_chip(i), peer(u, 0)
        at = lam_ref.at[b, j]
        return remote(at, at, asend.at[0], arecv.at[i, u], j, b)

    for i in range(1, chips):
        first_copy(i, 0).start()

    @pl.loop(1, groups)
    def _(u):
        for i in range(chips):
            first_copy(i, u).start()

    total_of(tab.at[pl.ds(0, cols - 1)], tsend.at[0], trecv.at[0]).wait_recv()

    def halves(full):
        high = full.astype(jnp.bfloat16).astype(jnp.float32)
        return high, full - high

    def twice(pieces):
        whole = jnp.concatenate([*pieces, jnp.ones((16, total_pts), jnp.float32)], axis=0).astype(jnp.bfloat16)
        return jnp.concatenate([whole, whole], axis=1)

    span = GROUP * rows
    pad = (lhs_own.shape[0] - 16) // 2
    lhs[...] = twice(halves(jnp.concatenate(
        [jnp.concatenate([tab[t, n] for n in range(GROUP)], axis=0) for t in range(cols)], axis=1
    )))
    mine = jnp.concatenate([tab[t, member] for t in range(cols)], axis=1)
    if pad > rows:
        mine = jnp.concatenate([mine, jnp.zeros((pad - rows, total_pts), jnp.float32)], axis=0)
    lhs_own[...] = twice(halves(mine))

    def lanes(q):
        return pl.ds(pl.multiple_of(q * part, LANES), part)

    def weighted(left, b, j, r):
        lam_t = jnp.concatenate([lam_ref[b, j, pl.ds(r + n, 1)] for n in range(2)], axis=1) * LOG2E
        cur_t = jnp.concatenate([curve[b, j, pl.ds(r + n, 1)] for n in range(2)], axis=1) * LOG2E
        c = consts[0]
        e = jnp.exp2(c * (lam_t + cur_t * c))
        ratio = jnp.exp2(wide * lam_t + cur_t * consts[1])
        turn = jnp.broadcast_to(jnp.exp2(cur_t * (2.0 * wide * wide)), e.shape)
        highs, lows = [], []
        steps = total_pts // STRIDE
        for m in range(steps):
            e_hi = e.astype(jnp.bfloat16)
            highs.append(e_hi)
            lows.append((e - e_hi.astype(jnp.float32)).astype(jnp.bfloat16))
            if m < steps - 1:
                e = e * ratio
            if m < steps - 2:
                ratio = ratio * turn
        return jnp.dot(left[...], jnp.concatenate(highs + lows, axis=0), preferred_element_type=jnp.float32)

    def compute(item, b, j, q):
        for t in range(part_rows // 2):
            acc = weighted(lhs, b, j, q * part_rows + t * 2)
            inv = 1.0 / acc[2 * span:2 * span + 8]
            at = pl.ds(t * 2 * LANES, 2 * LANES)
            for n in range(GROUP):
                value = acc[n * rows:(n + 1) * rows] + acc[span + n * rows:span + (n + 1) * rows]
                stage[item, n, :, at] = value * inv[:rows]
        species[b, j, :, lanes(q)] = stage[item, member]

    def local(b, j):
        for t in range(part_rows // 2):
            acc = weighted(lhs_own, b, j, t * 2)
            inv = 1.0 / acc[2 * pad:2 * pad + 8]
            species[b, j, :, pl.ds(t * 2 * LANES, 2 * LANES)] = (acc[:rows] + acc[pad:pad + rows]) * inv[:rows]
        hand_on(b, j, 0)

    def member_copy(item, d, b, j, q):
        to = lax.rem(member + d, GROUP)
        return remote(stage.at[item, to], species.at[b, j, :, lanes(q)], msend.at[0], mrecv.at[item, member], group * GROUP + to, me)

    def member_arrival(item, d, b, j, q):
        at = species.at[b, j, :, lanes(q)]
        return remote(at, at, msend.at[0], mrecv.at[item, lax.rem(member + d, GROUP)], col, partner)

    def y_copy(i, j, q):
        at = species.at[me, j, :, lanes(q)]
        return remote(at, at, ysend.at[0], yrecv.at[chips - 1 - i, j, q - (PARTS - SINGLE)], col, other_chip(i))

    def y_arrival(i, j, q):
        at = species.at[other_chip(i), j, :, lanes(q)]
        return remote(at, at, ysend.at[0], yrecv.at[i - 1, j, q - (PARTS - SINGLE)], col, other_chip(i))

    def hand_on(b, j, q):
        at = species.at[b, j, :, lanes(q)]
        remote(at, at, psend.at[0], precv.at[0], col, partner).start()

    def second_copy(u, i, d):
        at = lam_ref.at[other_chip(i), peer(u, 0), pl.ds(0, part_rows)]
        return remote(at, at, bsend.at[0], brecv.at[u, member], peer(0, d), me)

    def second_arrival(u, d):
        at = lam_ref.at[pl.ds(0, chips), 0, pl.ds(0, part_rows)]
        return remote(at, at, bsend.at[0], brecv.at[u, lax.rem(member + d, GROUP)], col, partner)

    def rest_copy(u, i, d):
        at = lam_ref.at[other_chip(i), peer(u, 0), pl.ds(part_rows, sub - part_rows)]
        return remote(at, at, rsend.at[0], rrecv.at[0], peer(0, d), me)

    def single_item(u, k):
        item = u * SINGLE + k
        q = PARTS - SINGLE + k
        j = peer(u, 0)
        compute(item, me, j, q)
        for d in range(1, GROUP):
            member_copy(item, d, me, j, q).start()
        for i in range(1, chips):
            y_copy(i, j, q).start()
        hand_on(me, j, q)

    def double_item(u, i):
        item = singles + u * chips + i
        b, j = other_chip(i), peer(u, 0)
        compute(item, b, j, 1)
        for d in range(1, GROUP):
            member_copy(item, d, b, j, 1).start()
        hand_on(b, j, 1)

    @pl.loop(0, groups)
    def _(u):
        @pl.when(u > 0)
        def _():
            first_arrival(0, u).wait_recv()

        @pl.loop(0, SINGLE)
        def _(k):
            single_item(u, k)

        for i in range(1, chips):
            first_arrival(i, u).wait_recv()

        @pl.when(u == 0)
        def _():
            total_of(curve.at[pl.ds(0, chips - 1), :, pl.ds(0, 2 * part_rows)], ksend.at[0], krecv.at[0]).wait_recv()

        for i in range(chips):
            for d in range(1, GROUP):
                second_copy(u, i, d).start()

        @pl.loop(0, chips)
        def _(i):
            double_item(u, i)
            local(other_chip(i), peer(u, 0))

        for k in range(SINGLE):
            for d in range(1, GROUP):
                q = PARTS - SINGLE + k
                j = peer(u, d)
                member_arrival(u * SINGLE + k, d, me, j, q).wait_recv()
                for i in range(1, chips):
                    y_copy(i, j, q).start()
                hand_on(me, j, q)

    @pl.loop(0, groups)
    def _(u):
        for i in range(chips):
            for d in range(1, GROUP):
                rest_copy(u, i, d).start()

    def y_arrivals(u, d):
        for k in range(SINGLE):
            for i in range(1, chips):
                q = PARTS - SINGLE + k
                y_arrival(i, peer(u, d), q).wait_recv()
                hand_on(other_chip(i), peer(u, d), q)

    @pl.loop(0, groups)
    def _(u):
        @pl.loop(1, GROUP)
        def _(d):
            second_arrival(u, d).wait_recv()

            @pl.loop(0, chips)
            def _(i):
                b, j = other_chip(i), peer(u, d)
                local(b, j)
                member_arrival(singles + u * chips + i, d, b, j, 1).wait_recv()
                hand_on(b, j, 1)

            @pl.when(u > 0)
            def _():
                y_arrivals(u - 1, d)

    total_of(lam_ref.at[pl.ds(0, chips), pl.ds(0, (GROUP - 1) * groups), pl.ds(part_rows, sub - part_rows)], rsend.at[0], rrecv.at[0]).wait_recv()
    for i in range(chips):
        at = lam_ref.at[other_chip(i)]
        remote(at, at, lsend.at[0], lrecv.at[0], col, partner).start()

    @pl.loop(0, groups)
    def _(u):
        y_arrivals(u, 0)

    @pl.loop(1, GROUP)
    def _(d):
        y_arrivals(groups - 1, d)

    total_of(tab.at[pl.ds(0, cols - 1)], tsend.at[0], trecv.at[0]).wait_send()
    total_of(curve.at[pl.ds(0, chips - 1), :, pl.ds(0, 2 * part_rows)], ksend.at[0], krecv.at[0]).wait_send()
    total_of(lam_ref.at[0, pl.ds(0, chips * groups - 1)], asend.at[0], lrecv.at[0]).wait_send()
    spread = pl.ds(0, (GROUP - 1) * groups)
    total_of(lam_ref.at[pl.ds(0, chips), spread, pl.ds(0, part_rows)], bsend.at[0], lrecv.at[0]).wait_send()
    total_of(lam_ref.at[pl.ds(0, chips), spread, pl.ds(part_rows, sub - part_rows)], rsend.at[0], lrecv.at[0]).wait_send()
    total_of(stage.at[:, pl.ds(0, GROUP - 1)], msend.at[0], precv.at[0]).wait_send()
    total_of(species.at[pl.ds(0, chips - 1), :, :, pl.ds(0, SINGLE * part)], ysend.at[0], precv.at[0]).wait_send()
    total_of(lam_ref.at[pl.ds(0, chips)], lsend.at[0], lrecv.at[0]).wait()
    total_of(species.at[pl.ds(0, chips)], psend.at[0], precv.at[0]).wait()


def write_kernel(species, lam, out_ref, lam_out, sem):
    bins, cols, _, width = species.shape
    for b in range(bins):
        for j in range(cols):
            pltpu.make_async_copy(species.at[b, j], out_ref.at[:, pl.ds((b * cols + j) * width, width)], sem.at[0]).start()
    keep = pltpu.make_async_copy(lam, lam_out, sem.at[1])
    keep.start()
    pltpu.make_async_copy(out_ref, out_ref, sem.at[0]).wait()
    keep.wait()


def per_device(slope, curvature, target_mean, target_var, table):
    cols = lax.axis_size("col")
    bins = lax.axis_size("bin")
    all_species, pts = table.shape
    rows = all_species // cols
    pad = -(-rows // 8) * 8
    total_pts = pts * cols
    per_shard = slope.shape[0]
    sub = per_shard // cols // LANES
    width = sub * LANES
    chips = bins // 2
    groups = cols // GROUP
    items = groups * (SINGLE + chips)

    def blocks(a):
        return a.reshape(cols, sub, LANES)

    placed = table.reshape(cols, rows, pts)
    vmem = pl.BlockSpec(memory_space=pltpu.VMEM)
    hbm = pl.BlockSpec(memory_space=pltpu.HBM)
    dma = pltpu.SemaphoreType.DMA
    one = dma((1,))
    species, lam = pl.pallas_call(
        functools.partial(kernel, cols, bins, total_pts, rows),
        out_shape=(
            jax.ShapeDtypeStruct((bins, cols, rows, width), jnp.float32),
            jax.ShapeDtypeStruct((bins, cols, sub, LANES), jnp.float32),
        ),
        in_specs=[hbm] * 5,
        out_specs=(vmem, vmem),
        scratch_shapes=[
            pltpu.VMEM((3, sub, LANES), jnp.float32),
            pltpu.VMEM((bins, cols, sub, LANES), jnp.float32),
            pltpu.VMEM((cols, rows, pts), jnp.float32),
            pltpu.VMEM((cols, GROUP, rows, pts), jnp.float32),
            pltpu.VMEM((2 * GROUP * rows + 16, 2 * total_pts), jnp.bfloat16),
            pltpu.VMEM((2 * pad + 16, 2 * total_pts), jnp.bfloat16),
            pltpu.VMEM((2, STRIDE, 2 * LANES), jnp.float32),
            pltpu.VMEM((items, GROUP, rows, width // PARTS), jnp.float32),
            dma((5,)), pltpu.SemaphoreType.REGULAR,
            one, one, one, one, one, dma((chips, groups)),
            one, dma((groups, GROUP)), one, one,
            one, one, one, dma((items, GROUP)),
            one, dma((chips - 1, cols, SINGLE)), one, one,
        ],
        compiler_params=pltpu.CompilerParams(collective_id=0, has_side_effects=True, vmem_limit_bytes=24 << 20),
    )(*[
        pltpu.with_memory_space_constraint(a, pltpu.HBM)
        for a in (blocks(slope), blocks(curvature), blocks(target_mean), blocks(target_var), placed)
    ])
    species_mean, lam = pl.pallas_call(
        write_kernel,
        out_shape=(
            jax.ShapeDtypeStruct((rows, per_shard * bins), jnp.float32),
            jax.ShapeDtypeStruct((bins, cols, sub, LANES), jnp.float32),
        ),
        in_specs=[vmem, vmem],
        out_specs=(hbm, hbm),
        scratch_shapes=[dma((2,))],
        compiler_params=pltpu.CompilerParams(vmem_limit_bytes=4 << 20),
    )(species, lam)
    return species_mean, lam.reshape(-1)


def solution(mesh):
    placed = (P("bin"), P("bin"), P("bin"), P("bin"), P(None, "col"))
    return jax.shard_map(
        per_device, mesh=mesh, in_specs=placed, out_specs=(P("col", None), P()), check_vma=False
    )
```

time: 43.7 us -> 36.2 us (0.83)
  the two profiles are of different devices: /device:TPU:0 before, /device:TPU:19 now
where the time goes in v1:
time: 36.2 us; the launch traced here: 36.1 us
  Pallas kernels  35.4 us (98%)
  between operations  0.64 us (2%)
    pallas_call x1, Pallas kernels, per_device(): pl.pallas_call(functools.partial(kernel, cols, bins, total_pts, rows), ou...  33.3 us
    pallas_call x1, Pallas kernels, per_device(): pl.pallas_call(write_kernel, out_shape=(jax.ShapeDtypeStruct((rows, per_s...  2.18 us

profile of v1, /device:TPU:19, one launch (start us, length us, event | category | flops | bytes accessed | tf_op | source)
XLA Modules:
  0.0 36.1 jit_solution(1160052113535186989)
XLA Ops:
  0.6 33.3 %shard_map.68 = (f32[4,8,8,4096]{3,2,1,0:T(8,128)S(1)}, f32[4,8,32,128]{3,2,1,0:T(8,128)S(1)}) custom-call(f32[8,32,128]{2,1,0:T(8,128)} %bitcast.6, f32[8,32,128]{2,1,0:T(8,128)} %bitcast.7, f32[8,32,128]{2,1,0:T(8,128)} %bitcast.8, f32[8,32,128]{2,1,0:T(8,128)} %bitcast.9, f32[8,8,64]{2,1,0:T(8,128)} %bitcast.10), custom_call_target="tpu_custom_call" | custom-call | tf_op jit(solution)/shard_map/pallas_call | solution.py:430
  33.9 2.2 %shard_map.69 = (f32[8,131072]{1,0:T(8,128)}, f32[4,8,32,128]{3,2,1,0:T(8,128)}) custom-call(f32[4,8,8,4096]{3,2,1,0:T(8,128)S(1)} %get-tuple-element.6.species, f32[4,8,32,128]{3,2,1,0:T(8,128)S(1)} %get-tuple-element.7.lam), custom_call_target="tpu_custom_call" | custom-call | tf_op jit(solution)/shard_map/pallas_call | solution.py:458

commit v2 on v1

v2 whole, which is shorter than its diff:
```python
import functools
import math
import jax
import jax.numpy as jnp
from jax import lax
from jax.experimental import pallas as pl
from jax.experimental.pallas import tpu as pltpu
from jax.sharding import PartitionSpec as P

ITERS = 3
LANES = 128
LOG2E = math.log2(math.e)
MESH = pl.DeviceIdType.MESH
UNROLL = 32
STRIDE = 32
DEPTH = 256
GROUP = 4
PARTS = 4
SINGLE = 2


def kernel(
    cols, bins, total_pts, rows,
    slope_hbm, curve_hbm, mean_hbm, var_hbm, placed_hbm,
    species, lam_ref,
    own, curve, placed, packed, tab, lhs, lhs_own, consts, stage,
    isem, far, tsend, trecv, ksend, krecv, asend, arecv, bsend, brecv,
    lsend, lrecv, msend, mrecv, ysend, yrecv, psend, precv,
    sums,
):
    col = lax.axis_index("col")
    me = lax.axis_index("bin")
    core = lax.rem(me, 2)
    partner = me + 1 - 2 * core
    chips = bins // 2
    groups = cols // GROUP
    member = lax.rem(col, GROUP)
    group = col // GROUP
    last = groups - 1
    sub = own.shape[1]
    width = sub * LANES
    part = width // PARTS
    part_rows = sub // PARTS
    pts = total_pts // cols
    side = packed.shape[3] // pts
    per = SINGLE + chips
    blocks = part_rows // 2
    lag = blocks % 2 == 0
    sums_group, sums_own = sums

    def other_chip(i):
        return lax.rem(me + 2 * i, bins)

    def peer(u, d):
        return lax.rem(group + u, groups) * GROUP + lax.rem(member + d, GROUP)

    def remote(src, dst, send, recv, c, b):
        return pltpu.make_async_remote_copy(
            src_ref=src, dst_ref=dst, send_sem=send, recv_sem=recv,
            device_id=(c, b), device_id_type=MESH,
        )

    def total_of(ref, send, recv):
        return remote(ref, ref, send, recv, col, partner)

    def greet(sem, c, b):
        pl.semaphore_signal(sem, inc=1, device_id=(c, b), device_id_type=MESH)

    barrier = pltpu.get_barrier_semaphore()
    greet(barrier, col, partner)
    for d in range(1, GROUP):
        greet(barrier, peer(0, d), me)
    for i in range(1, chips):
        greet(barrier, col, other_chip(i))

    def greet_group(sem, g):
        for d in range(GROUP):
            greet(sem, g * GROUP + d, me)
        for i in range(1, chips):
            greet(sem, g * GROUP + member, other_chip(i))

    @pl.loop(group + 1, groups)
    def _(g):
        greet_group(barrier, g)

    load_table = pltpu.make_async_copy(placed_hbm, placed, isem.at[4])
    load_table.start()
    loads = [
        pltpu.make_async_copy(a.at[col], own.at[n], isem.at[n])
        for n, a in enumerate((slope_hbm, mean_hbm, var_hbm))
    ]
    loads.append(pltpu.make_async_copy(curve_hbm, curve.at[me], isem.at[3]))
    for load in loads:
        load.start()

    for pair in (*sums_group, *sums_own):
        for acc in pair:
            pltpu.matmul_pop(acc)

    each = GROUP + chips - 1
    h = 1.0 / total_pts
    wide = STRIDE * h
    first = (lax.broadcasted_iota(jnp.int32, consts.shape[1:], 0).astype(jnp.float32) + 0.5) * h
    consts[0] = first
    consts[1] = wide * (2.0 * first + wide)

    load_table.wait()
    for g in range(groups):
        for p in range(GROUP // side):
            packed[g, p] = jnp.concatenate([placed[g * GROUP + p * side + n] for n in range(side)], axis=1)

    def table_copy(to):
        return remote(packed.at[to // GROUP], tab.at[col], tsend.at[0], trecv.at[0], to, me)

    def curve_copy(i):
        at = curve.at[me, :, pl.ds(0, 2 * part_rows)]
        return remote(at, at, ksend.at[0], krecv.at[0], col, other_chip(i))

    def enter():
        pl.semaphore_wait(barrier, (group + 1) * each)

        @pl.loop(0, group)
        def _(g):
            greet_group(far, g)

        @pl.loop(0, group)
        def _(g):
            for d in range(GROUP):
                table_copy(g * GROUP + d).start()

        for d in range(1, GROUP):
            table_copy(peer(0, d)).start()
        tab[col] = packed[group]

    for load in loads:
        load.wait()

    @pl.when(group == last)
    def _():
        enter()
        for i in range(1, chips):
            curve_copy(i).start()

    curve2 = curve[me, col] * LOG2E
    target = own[1]
    var = own[2]
    lam = own[0]
    bend = jnp.exp2(curve2 * (2.0 * h * h))

    def newton(lam):
        lam2 = lam * LOG2E

        def begin(g):
            c = ((g * UNROLL).astype(jnp.float32) + 0.5) * h
            return jnp.exp2(c * (lam2 + curve2 * c)), jnp.exp2(h * (lam2 + curve2 * (2.0 * c + h)))

        def body(g, carry):
            total, mom, e, ratio = carry
            later = begin(g + 1)
            c = ((g * UNROLL).astype(jnp.float32) + 0.5) * h
            run = e
            runs = e
            for i in range(1, UNROLL):
                e = e * ratio
                if i < UNROLL - 1:
                    ratio = ratio * bend
                run = run + e
                runs = runs + run
            return total + run, mom + (c * run + h * (UNROLL * run - runs)), *later

        zero = jnp.zeros_like(lam)
        total, mom, _, _ = lax.fori_loop(0, total_pts // UNROLL, body, (zero, zero, *begin(jnp.int32(0))))
        return lam + (target - mom / total) / var

    for step in range(ITERS):
        lam = newton(lam)
    lam_ref[me, col] = lam

    @pl.when(group < last)
    def _():
        enter()

    def first_copy(i, u):
        at = lam_ref.at[me, col]
        return remote(at, at, asend.at[0], arecv.at[(chips - i) % chips, lax.rem(groups - u, groups)], peer(u, 0), other_chip(i))

    def first_arrival(i, u):
        b, j = other_chip(i), peer(u, 0)
        at = lam_ref.at[b, j]
        return remote(at, at, asend.at[0], arecv.at[i, u], j, b)

    def second_copy(u, i, d):
        at = lam_ref.at[other_chip(i), peer(u, 0)]
        return remote(at, at, bsend.at[0], brecv.at[u, member], peer(0, d), me)

    def second_arrival(u, d):
        at = lam_ref.at[pl.ds(0, chips), 0]
        return remote(at, at, bsend.at[0], brecv.at[u, lax.rem(member + d, GROUP)], col, partner)

    for i in range(1, chips):
        first_copy(i, 0).start()
    for d in range(1, GROUP):
        second_copy(0, 0, d).start()

    @pl.when(group < last)
    def _():
        for i in range(1, chips):
            curve_copy(i).start()
        pl.semaphore_wait(far, (last - group) * each)

        @pl.loop(group + 1, groups)
        def _(g):
            for d in range(GROUP):
                table_copy(g * GROUP + d).start()

    @pl.loop(1, groups)
    def _(u):
        for i in range(chips):
            first_copy(i, u).start()

    total_of(tab.at[pl.ds(0, cols - 1)], tsend.at[0], trecv.at[0]).wait_recv()

    def split(full):
        high = full.astype(jnp.bfloat16).astype(jnp.float32)
        return jnp.concatenate([high, full - high, jnp.ones((16, total_pts), jnp.float32)], axis=0).astype(jnp.bfloat16)

    def gathered(n):
        return jnp.concatenate([tab[t, n // side][:, n % side * pts:(n % side + 1) * pts] for t in range(cols)], axis=1)

    span = GROUP * rows
    pad = (lhs_own.shape[0] - 16) // 2
    every = [gathered(n) for n in range(GROUP)]
    lhs[...] = split(jnp.concatenate(every, axis=0))
    mine = every[0]
    for n in range(1, GROUP):
        mine = jnp.where(member == n, every[n], mine)
    if pad > rows:
        mine = jnp.concatenate([mine, jnp.zeros((pad - rows, total_pts), jnp.float32)], axis=0)
    lhs_own[...] = split(mine)

    def lanes(q):
        return pl.ds(pl.multiple_of(q * part, LANES), part)

    def push(left, accs, b, j, r):
        lam_t = jnp.concatenate([lam_ref[b, j, pl.ds(r + n, 1)] for n in range(2)], axis=1) * LOG2E
        cur_t = jnp.concatenate([curve[b, j, pl.ds(r + n, 1)] for n in range(2)], axis=1) * LOG2E
        c = consts[0]
        e = jnp.exp2(c * (lam_t + cur_t * c))
        ratio = jnp.exp2(wide * lam_t + cur_t * consts[1])
        turn = jnp.broadcast_to(jnp.exp2(cur_t * (2.0 * wide * wide)), e.shape)
        steps = DEPTH // STRIDE
        tiles = total_pts // DEPTH
        for n in range(tiles):
            highs, lows = [], []
            for m in range(steps):
                e_hi = e.astype(jnp.bfloat16)
                highs.append(e_hi)
                lows.append((e - e_hi.astype(jnp.float32)).astype(jnp.bfloat16))
                if n < tiles - 1 or m < steps - 1:
                    e = e * ratio
                    ratio = ratio * turn
            for q, pieces in enumerate((highs, lows)):
                pltpu.matmul_push_rhs(jnp.concatenate(pieces, axis=0), n % 2, q)
            piece = left[:, n * DEPTH:(n + 1) * DEPTH]
            for acc in accs:
                pltpu.matmul_acc_lhs(acc, piece, load_staged_rhs=n % 2)

    def pick(t):
        return (blocks - t) % 2

    def at_block(t):
        return pl.ds(t * 2 * LANES, 2 * LANES)

    def run(start, done, sent, before=None):
        for t in range(blocks):
            start(t)
            if t > 0:
                done(t - 1)
            elif before is not None:
                before()
        if not lag:
            done(blocks - 1)
            sent()

    def close(done, sent):
        if lag:
            done(blocks - 1)
            sent()

    def hand_on(b, j, q):
        at = species.at[b, j, :, lanes(q)]
        remote(at, at, psend.at[0], precv.at[0], col, partner).start()

    def member_copy(item, d, b, j, q):
        to = lax.rem(member + d, GROUP)
        return remote(stage.at[item, to], species.at[b, j, :, lanes(q)], msend.at[0], mrecv.at[item], group * GROUP + to, me)

    def member_arrivals(item):
        total_of(species.at[0, pl.ds(0, GROUP - 1), :, pl.ds(0, part)], msend.at[0], mrecv.at[item]).wait_recv()

    def y_copy(i, u, d, k):
        at = species.at[me, peer(u, d), :, lanes(PARTS - SINGLE + k)]
        return remote(at, at, ysend.at[0], yrecv.at[chips - 1 - i, u, k], col, other_chip(i))

    def y_arrivals(u, k):
        for i in range(1, chips):
            total_of(species.at[0, pl.ds(0, GROUP), :, pl.ds(0, part)], ysend.at[0], yrecv.at[i - 1, u, k]).wait_recv()
            for d in range(GROUP):
                hand_on(other_chip(i), peer(u, d), PARTS - SINGLE + k)

    def group_item(u, r):
        item = u * per + r
        b = me if r < SINGLE else other_chip(r - SINGLE)
        q = PARTS - SINGLE + r if r < SINGLE else 1
        j = peer(u, 0)

        def start(t):
            push(lhs, sums_group[pick(t)], b, j, q * part_rows + t * 2)

        def done(t):
            one, two = sums_group[pick(t)]
            acc = pltpu.matmul_pop(one) + pltpu.matmul_pop(two)
            inv = 1.0 / acc[2 * span:2 * span + 8]
            for n in range(GROUP):
                value = acc[n * rows:(n + 1) * rows] + acc[span + n * rows:span + (n + 1) * rows]
                stage[item, n, :, at_block(t)] = value * inv[:rows]

        def sent():
            species[b, j, :, lanes(q)] = stage[item, member]
            for d in range(1, GROUP):
                member_copy(item, d, b, j, q).start()
            if r < SINGLE:
                for i in range(1, chips):
                    y_copy(i, u, 0, r).start()
            hand_on(b, j, q)

        return start, done, sent

    def single_arrivals(u, k):
        member_arrivals(u * per + k)
        for d in range(1, GROUP):
            for i in range(1, chips):
                y_copy(i, u, d, k).start()
            hand_on(me, peer(u, d), PARTS - SINGLE + k)

    def double_arrivals(u, i):
        member_arrivals(u * per + SINGLE + i)
        for d in range(1, GROUP):
            hand_on(other_chip(i), peer(u, d), 1)

    locals_each = GROUP * chips

    def local_item(u, k):
        b, j = other_chip(lax.rem(k, chips)), peer(u, k // chips)

        def start(t):
            push(lhs_own, sums_own[pick(t)], b, j, t * 2)

        def done(t):
            one, two = sums_own[pick(t)]
            acc = pltpu.matmul_pop(one) + pltpu.matmul_pop(two)
            inv = 1.0 / acc[2 * pad:2 * pad + 8]
            species[b, j, :, at_block(t)] = (acc[:rows] + acc[pad:pad + rows]) * inv[:rows]

        return start, done, lambda: hand_on(b, j, 0)

    @pl.loop(0, groups)
    def _(u):
        @pl.when(u > 0)
        def _():
            first_arrival(0, u).wait_recv()
            for d in range(1, GROUP):
                second_copy(u, 0, d).start()

        before = None
        for r in range(per):
            if r == 1:
                for i in range(1, chips):
                    first_arrival(i, u).wait_recv()
                    for d in range(1, GROUP):
                        second_copy(u, i, d).start()

                @pl.when(u == 0)
                def _():
                    total_of(curve.at[pl.ds(0, chips - 1), :, pl.ds(0, 2 * part_rows)], ksend.at[0], krecv.at[0]).wait_recv()

            start, done, sent = group_item(u, r)
            run(start, done, sent, before)
            before = functools.partial(close, done, sent)
        before()

        run(*local_item(u, 0))
        for d in range(GROUP):
            if d > 0:
                second_arrival(u, d).wait_recv()

            @pl.loop(max(1, d * chips), (d + 1) * chips)
            def _(k):
                _, done, sent = local_item(u, k - 1)
                run(*local_item(u, k), before=functools.partial(close, done, sent))

            @pl.when(u > 0)
            def _():
                if d < 2:
                    for i in range(d * chips // 2, (d + 1) * chips // 2):
                        double_arrivals(u - 1, i)
                if d % 2 == 1:
                    y_arrivals(u - 1, d // 2)

            if d > 1:
                single_arrivals(u, d - 2)

        _, done, sent = local_item(u, locals_each - 1)
        close(done, sent)

    for i in range(chips):
        at = lam_ref.at[other_chip(i)]
        remote(at, at, lsend.at[0], lrecv.at[0], col, partner).start()

    for i in range(chips):
        double_arrivals(last, i)
    for s in range(SINGLE):
        y_arrivals(last, s)

    total_of(tab.at[pl.ds(0, cols - 1)], tsend.at[0], trecv.at[0]).wait_send()
    total_of(curve.at[pl.ds(0, chips - 1), :, pl.ds(0, 2 * part_rows)], ksend.at[0], krecv.at[0]).wait_send()
    total_of(lam_ref.at[0, pl.ds(0, chips * groups - 1)], asend.at[0], lrecv.at[0]).wait_send()
    total_of(lam_ref.at[pl.ds(0, chips), pl.ds(0, (GROUP - 1) * groups)], bsend.at[0], lrecv.at[0]).wait_send()
    total_of(stage.at[:, pl.ds(0, GROUP - 1)], msend.at[0], precv.at[0]).wait_send()
    total_of(species.at[pl.ds(0, chips - 1), :, :, pl.ds(0, SINGLE * part)], ysend.at[0], precv.at[0]).wait_send()
    total_of(lam_ref.at[pl.ds(0, chips)], lsend.at[0], lrecv.at[0]).wait()
    total_of(species.at[pl.ds(0, chips)], psend.at[0], precv.at[0]).wait()


def scoped_kernel(cols, bins, total_pts, rows, pad, *refs):
    def pair(m):
        return tuple(pltpu.ACC(q)((m, 256), jnp.float32) for q in range(2))

    def body(sums):
        kernel(cols, bins, total_pts, rows, *refs, sums)

    shapes = tuple((pair(m), pair(m)) for m in (2 * GROUP * rows + 16, 2 * pad + 16))
    pl.run_scoped(body, shapes)


def write_kernel(species, lam, out_ref, lam_out, sem):
    bins, cols, _, width = species.shape
    for b in range(bins):
        for j in range(cols):
            pltpu.make_async_copy(species.at[b, j], out_ref.at[:, pl.ds((b * cols + j) * width, width)], sem.at[0]).start()
    keep = pltpu.make_async_copy(lam, lam_out, sem.at[1])
    keep.start()
    pltpu.make_async_copy(out_ref, out_ref, sem.at[0]).wait()
    keep.wait()


def per_device(slope, curvature, target_mean, target_var, table):
    cols = lax.axis_size("col")
    bins = lax.axis_size("bin")
    all_species, pts = table.shape
    rows = all_species // cols
    pad = -(-rows // 8) * 8
    total_pts = pts * cols
    per_shard = slope.shape[0]
    sub = per_shard // cols // LANES
    width = sub * LANES
    chips = bins // 2
    groups = cols // GROUP
    items = groups * (SINGLE + chips)
    side = max(1, min(GROUP, LANES // pts))
    packed = (groups, GROUP // side, rows, side * pts)

    def blocks(a):
        return a.reshape(cols, sub, LANES)

    placed = table.reshape(cols, rows, pts)
    vmem = pl.BlockSpec(memory_space=pltpu.VMEM)
    hbm = pl.BlockSpec(memory_space=pltpu.HBM)
    dma = pltpu.SemaphoreType.DMA
    one = dma((1,))
    species, lam = pl.pallas_call(
        functools.partial(scoped_kernel, cols, bins, total_pts, rows, pad),
        out_shape=(
            jax.ShapeDtypeStruct((bins, cols, rows, width), jnp.float32),
            jax.ShapeDtypeStruct((bins, cols, sub, LANES), jnp.float32),
        ),
        in_specs=[hbm] * 5,
        out_specs=(vmem, vmem),
        scratch_shapes=[
            pltpu.VMEM((3, sub, LANES), jnp.float32),
            pltpu.VMEM((bins, cols, sub, LANES), jnp.float32),
            pltpu.VMEM((cols, rows, pts), jnp.float32),
            pltpu.VMEM(packed, jnp.float32),
            pltpu.VMEM((cols, *packed[1:]), jnp.float32),
            pltpu.VMEM((2 * GROUP * rows + 16, total_pts), jnp.bfloat16),
            pltpu.VMEM((2 * pad + 16, total_pts), jnp.bfloat16),
            pltpu.VMEM((2, STRIDE, 2 * LANES), jnp.float32),
            pltpu.VMEM((items, GROUP, rows, width // PARTS), jnp.float32),
            dma((5,)), pltpu.SemaphoreType.REGULAR,
            one, one, one, one, one, dma((chips, groups)),
            one, dma((groups, GROUP)),
            one, one, one, dma((items,)),
            one, dma((chips - 1, groups, SINGLE)), one, one,
        ],
        compiler_params=pltpu.CompilerParams(collective_id=0, has_side_effects=True, vmem_limit_bytes=24 << 20),
    )(*[
        pltpu.with_memory_space_constraint(a, pltpu.HBM)
        for a in (blocks(slope), blocks(curvature), blocks(target_mean), blocks(target_var), placed)
    ])
    species_mean, lam = pl.pallas_call(
        write_kernel,
        out_shape=(
            jax.ShapeDtypeStruct((rows, per_shard * bins), jnp.float32),
            jax.ShapeDtypeStruct((bins, cols, sub, LANES), jnp.float32),
        ),
        in_specs=[vmem, vmem],
        out_specs=(hbm, hbm),
        scratch_shapes=[dma((2,))],
        compiler_params=pltpu.CompilerParams(vmem_limit_bytes=4 << 20),
    )(species, lam)
    return species_mean, lam.reshape(-1)


def solution(mesh):
    placed = (P("bin"), P("bin"), P("bin"), P("bin"), P(None, "col"))
    return jax.shard_map(
        per_device, mesh=mesh, in_specs=placed, out_specs=(P("col", None), P()), check_vma=False
    )
```

time: 36.2 us -> 33.1 us (0.914)
  the two profiles are of different devices: /device:TPU:19 before, /device:TPU:0 now
where the time goes in v2:
time: 33.1 us; the launch traced here: 32.9 us
  Pallas kernels  32.3 us (98%)
  between operations  0.64 us (2%)
    pallas_call x1, Pallas kernels, per_device(): pl.pallas_call(functools.partial(scoped_kernel, cols, bins, total_pts, ro...  30.1 us
    pallas_call x1, Pallas kernels, per_device(): pl.pallas_call(write_kernel, out_shape=(jax.ShapeDtypeStruct((rows, per_s...  2.18 us

profile of v2, /device:TPU:0, one launch (start us, length us, event | category | flops | bytes accessed | tf_op | source)
XLA Modules:
  0.0 32.9 jit_solution(15035238287914428540)
XLA Ops:
  0.6 30.1 %shard_map.68 = (f32[4,8,8,4096]{3,2,1,0:T(8,128)S(1)}, f32[4,8,32,128]{3,2,1,0:T(8,128)S(1)}) custom-call(f32[8,32,128]{2,1,0:T(8,128)} %bitcast.6, f32[8,32,128]{2,1,0:T(8,128)} %bitcast.7, f32[8,32,128]{2,1,0:T(8,128)} %bitcast.8, f32[8,32,128]{2,1,0:T(8,128)} %bitcast.9, f32[8,8,64]{2,1,0:T(8,128)} %bitcast.10), custom_call_target="tpu_custom_call" | custom-call | tf_op jit(solution)/shard_map/pallas_call | solution.py:481
  30.8 2.2 %shard_map.69 = (f32[8,131072]{1,0:T(8,128)}, f32[4,8,32,128]{3,2,1,0:T(8,128)}) custom-call(f32[4,8,8,4096]{3,2,1,0:T(8,128)S(1)} %get-tuple-element.6.species, f32[4,8,32,128]{3,2,1,0:T(8,128)S(1)} %get-tuple-element.7.lam), custom_call_target="tpu_custom_call" | custom-call | tf_op jit(solution)/shard_map/pallas_call | solution.py:510

commit v3 on v2

--- a/solution.py
+++ b/solution.py
@@ -23,7 +23,7 @@
     cols, bins, total_pts, rows,
     slope_hbm, curve_hbm, mean_hbm, var_hbm, placed_hbm,
     species, lam_ref,
-    own, curve, placed, packed, tab, lhs, lhs_own, consts, stage,
+    own, curve, placed, packed, tab, lhs, consts, stage,
     isem, far, tsend, trecv, ksend, krecv, asend, arecv, bsend, brecv,
     lsend, lrecv, msend, mrecv, ysend, yrecv, psend, precv,
     sums,
@@ -46,7 +46,6 @@
     per = SINGLE + chips
     blocks = part_rows // 2
     lag = blocks % 2 == 0
-    sums_group, sums_own = sums
 
     def other_chip(i):
         return lax.rem(me + 2 * i, bins)
@@ -93,7 +92,7 @@
     for load in loads:
         load.start()
 
-    for pair in (*sums_group, *sums_own):
+    for pair in sums:
         for acc in pair:
             pltpu.matmul_pop(acc)
 
@@ -144,7 +143,6 @@
     curve2 = curve[me, col] * LOG2E
     target = own[1]
     var = own[2]
-    lam = own[0]
     bend = jnp.exp2(curve2 * (2.0 * h * h))
 
     def newton(lam):
@@ -172,9 +170,7 @@
         total, mom, _, _ = lax.fori_loop(0, total_pts // UNROLL, body, (zero, zero, *begin(jnp.int32(0))))
         return lam + (target - mom / total) / var
 
-    for step in range(ITERS):
-        lam = newton(lam)
-    lam_ref[me, col] = lam
+    lam_ref[me, col] = lax.fori_loop(0, ITERS, lambda _, lam: newton(lam), own[0])
 
     @pl.when(group < last)
     def _():
@@ -228,15 +224,7 @@
         return jnp.concatenate([tab[t, n // side][:, n % side * pts:(n % side + 1) * pts] for t in range(cols)], axis=1)
 
     span = GROUP * rows
-    pad = (lhs_own.shape[0] - 16) // 2
-    every = [gathered(n) for n in range(GROUP)]
-    lhs[...] = split(jnp.concatenate(every, axis=0))
-    mine = every[0]
-    for n in range(1, GROUP):
-        mine = jnp.where(member == n, every[n], mine)
-    if pad > rows:
-        mine = jnp.concatenate([mine, jnp.zeros((pad - rows, total_pts), jnp.float32)], axis=0)
-    lhs_own[...] = split(mine)
+    lhs[...] = split(jnp.concatenate([gathered(n) for n in range(GROUP)], axis=0))
 
     def lanes(q):
         return pl.ds(pl.multiple_of(q * part, LANES), part)
@@ -271,22 +259,6 @@
     def at_block(t):
         return pl.ds(t * 2 * LANES, 2 * LANES)
 
-    def run(start, done, sent, before=None):
-        for t in range(blocks):
-            start(t)
-            if t > 0:
-                done(t - 1)
-            elif before is not None:
-                before()
-        if not lag:
-            done(blocks - 1)
-            sent()
-
-    def close(done, sent):
-        if lag:
-            done(blocks - 1)
-            sent()
-
     def hand_on(b, j, q):
         at = species.at[b, j, :, lanes(q)]
         remote(at, at, psend.at[0], precv.at[0], col, partner).start()
@@ -308,33 +280,61 @@
             for d in range(GROUP):
                 hand_on(other_chip(i), peer(u, d), PARTS - SINGLE + k)
 
-    def group_item(u, r):
-        item = u * per + r
-        b = me if r < SINGLE else other_chip(r - SINGLE)
-        q = PARTS - SINGLE + r if r < SINGLE else 1
-        j = peer(u, 0)
-
-        def start(t):
-            push(lhs, sums_group[pick(t)], b, j, q * part_rows + t * 2)
-
-        def done(t):
-            one, two = sums_group[pick(t)]
-            acc = pltpu.matmul_pop(one) + pltpu.matmul_pop(two)
-            inv = 1.0 / acc[2 * span:2 * span + 8]
-            for n in range(GROUP):
-                value = acc[n * rows:(n + 1) * rows] + acc[span + n * rows:span + (n + 1) * rows]
-                stage[item, n, :, at_block(t)] = value * inv[:rows]
-
-        def sent():
-            species[b, j, :, lanes(q)] = stage[item, member]
+    count = SINGLE + chips
+    doubles_from = groups * count
+    locals_from = doubles_from + groups * chips
+    others = (GROUP - 1) * chips
+    total = locals_from + groups * others
+    spare = groups * per
+
+    def place(n):
+        u0, r0 = n // count, lax.rem(n, count)
+        n1 = jnp.maximum(n - doubles_from, 0)
+        u1, i1 = n1 // chips, lax.rem(n1, chips)
+        n2 = jnp.maximum(n - locals_from, 0)
+        u2, m2 = n2 // others, lax.rem(n2, others)
+        single = jnp.logical_and(n < doubles_from, r0 < SINGLE)
+        double = jnp.logical_and(n >= doubles_from, n < locals_from)
+        late = n >= locals_from
+        u = jnp.where(late, u2, jnp.where(double, u1, u0))
+        i = jnp.where(late, lax.rem(m2, chips), jnp.where(double, i1, jnp.maximum(r0 - SINGLE, 0)))
+        b = other_chip(i)
+        j = peer(u, jnp.where(late, 1 + m2 // chips, 0))
+        q = jnp.where(single, PARTS - SINGLE + r0, jnp.where(double, 1, 0))
+        item = jnp.where(single, u * per + r0, jnp.where(double, u * per + SINGLE + i, spare))
+        return single, u, r0, b, j, q, item
+
+    def start(n, t):
+        _, _, _, b, j, q, _ = place(n)
+        push(lhs, sums[pick(t)], b, j, q * part_rows + t * 2)
+
+    def done(n, t):
+        item = place(n)[6]
+        one, two = sums[pick(t)]
+        acc = pltpu.matmul_pop(one) + pltpu.matmul_pop(two)
+        inv = 1.0 / acc[2 * span:2 * span + 8]
+        for g in range(GROUP):
+            value = acc[g * rows:(g + 1) * rows] + acc[span + g * rows:span + (g + 1) * rows]
+            stage[item, g, :, at_block(t)] = value * inv[:rows]
+
+    def keep(n):
+        _, _, _, b, j, q, item = place(n)
+        species[b, j, :, lanes(q)] = stage[item, member]
+
+    def sent(n):
+        single, u, r, b, j, q, item = place(n)
+
+        @pl.when(item < spare)
+        def _():
             for d in range(1, GROUP):
                 member_copy(item, d, b, j, q).start()
-            if r < SINGLE:
-                for i in range(1, chips):
-                    y_copy(i, u, 0, r).start()
-            hand_on(b, j, q)
-
-        return start, done, sent
+
+        @pl.when(single)
+        def _():
+            for i in range(1, chips):
+                y_copy(i, u, 0, r).start()
+
+        hand_on(b, j, q)
 
     def single_arrivals(u, k):
         member_arrivals(u * per + k)
@@ -348,33 +348,19 @@
         for d in range(1, GROUP):
             hand_on(other_chip(i), peer(u, d), 1)
 
-    locals_each = GROUP * chips
-
-    def local_item(u, k):
-        b, j = other_chip(lax.rem(k, chips)), peer(u, k // chips)
-
-        def start(t):
-            push(lhs_own, sums_own[pick(t)], b, j, t * 2)
-
-        def done(t):
-            one, two = sums_own[pick(t)]
-            acc = pltpu.matmul_pop(one) + pltpu.matmul_pop(two)
-            inv = 1.0 / acc[2 * pad:2 * pad + 8]
-            species[b, j, :, at_block(t)] = (acc[:rows] + acc[pad:pad + rows]) * inv[:rows]
-
-        return start, done, lambda: hand_on(b, j, 0)
-
-    @pl.loop(0, groups)
-    def _(u):
-        @pl.when(u > 0)
+    def ready(n):
+        @pl.when(n < doubles_from)
         def _():
-            first_arrival(0, u).wait_recv()
-            for d in range(1, GROUP):
-                second_copy(u, 0, d).start()
-
-        before = None
-        for r in range(per):
-            if r == 1:
+            u, r = n // count, lax.rem(n, count)
+
+            @pl.when(jnp.logical_and(r == 0, u > 0))
+            def _():
+                first_arrival(0, u).wait_recv()
+                for d in range(1, GROUP):
+                    second_copy(u, 0, d).start()
+
+            @pl.when(r == SINGLE + 1)
+            def _():
                 for i in range(1, chips):
                     first_arrival(i, u).wait_recv()
                     for d in range(1, GROUP):
@@ -384,63 +370,81 @@
                 def _():
                     total_of(curve.at[pl.ds(0, chips - 1), :, pl.ds(0, 2 * part_rows)], ksend.at[0], krecv.at[0]).wait_recv()
 
-            start, done, sent = group_item(u, r)
-            run(start, done, sent, before)
-            before = functools.partial(close, done, sent)
-        before()
-
-        run(*local_item(u, 0))
-        for d in range(GROUP):
-            if d > 0:
-                second_arrival(u, d).wait_recv()
-
-            @pl.loop(max(1, d * chips), (d + 1) * chips)
-            def _(k):
-                _, done, sent = local_item(u, k - 1)
-                run(*local_item(u, k), before=functools.partial(close, done, sent))
-
-            @pl.when(u > 0)
+        m = n - locals_from
+
+        @pl.when(jnp.logical_and(m >= 0, lax.rem(m, chips) == 0))
+        def _():
+            second_arrival(m // others, 1 + lax.rem(m, others) // chips).wait_recv()
+
+    events = (
+        (doubles_from, 2, groups * SINGLE, lambda e: single_arrivals(e // SINGLE, lax.rem(e, SINGLE))),
+        (locals_from + 4, 3, groups * SINGLE, lambda e: y_arrivals(e // SINGLE, lax.rem(e, SINGLE))),
+        (locals_from + 5, 2, groups * chips, lambda e: double_arrivals(e // chips, lax.rem(e, chips))),
+    )
+
+    def served(n):
+        for begin, every, number, event in events:
+            m = n - begin
+
+            @pl.when(jnp.logical_and(jnp.logical_and(m >= 0, m < number * every), lax.rem(m, every) == 0))
             def _():
-                if d < 2:
-                    for i in range(d * chips // 2, (d + 1) * chips // 2):
-                        double_arrivals(u - 1, i)
-                if d % 2 == 1:
-                    y_arrivals(u - 1, d // 2)
-
-            if d > 1:
-                single_arrivals(u, d - 2)
-
-        _, done, sent = local_item(u, locals_each - 1)
-        close(done, sent)
+                event(m // every)
+
+    @pl.loop(0, total)
+    def _(n):
+        ready(n)
+        back = jnp.maximum(n - 1, 0)
+        for t in range(blocks):
+            start(n, t)
+            if t > 0:
+                done(n, t - 1)
+            elif lag:
+                done(back, blocks - 1)
+                keep(back)
+        if lag:
+            @pl.when(n > 0)
+            def _():
+                sent(back)
+        else:
+            done(n, blocks - 1)
+            keep(n)
+            sent(n)
+        served(n)
+
+    if lag:
+        done(total - 1, blocks - 1)
+        keep(total - 1)
+        sent(total - 1)
 
     for i in range(chips):
         at = lam_ref.at[other_chip(i)]
         remote(at, at, lsend.at[0], lrecv.at[0], col, partner).start()
 
-    for i in range(chips):
-        double_arrivals(last, i)
-    for s in range(SINGLE):
-        y_arrivals(last, s)
+    for begin, every, number, event in reversed(events):
+        @pl.loop(max(0, min(number, -((begin - total) // every))), number)
+        def _(e):
+            event(e)
+
 
     total_of(tab.at[pl.ds(0, cols - 1)], tsend.at[0], trecv.at[0]).wait_send()
     total_of(curve.at[pl.ds(0, chips - 1), :, pl.ds(0, 2 * part_rows)], ksend.at[0], krecv.at[0]).wait_send()
     total_of(lam_ref.at[0, pl.ds(0, chips * groups - 1)], asend.at[0], lrecv.at[0]).wait_send()
     total_of(lam_ref.at[pl.ds(0, chips), pl.ds(0, (GROUP - 1) * groups)], bsend.at[0], lrecv.at[0]).wait_send()
-    total_of(stage.at[:, pl.ds(0, GROUP - 1)], msend.at[0], precv.at[0]).wait_send()
+    total_of(stage.at[pl.ds(0, spare), pl.ds(0, GROUP - 1)], msend.at[0], precv.at[0]).wait_send()
     total_of(species.at[pl.ds(0, chips - 1), :, :, pl.ds(0, SINGLE * part)], ysend.at[0], precv.at[0]).wait_send()
     total_of(lam_ref.at[pl.ds(0, chips)], lsend.at[0], lrecv.at[0]).wait()
     total_of(species.at[pl.ds(0, chips)], psend.at[0], precv.at[0]).wait()
 
 
-def scoped_kernel(cols, bins, total_pts, rows, pad, *refs):
+def scoped_kernel(cols, bins, total_pts, rows, *refs):
     def pair(m):
         return tuple(pltpu.ACC(q)((m, 256), jnp.float32) for q in range(2))
 
     def body(sums):
         kernel(cols, bins, total_pts, rows, *refs, sums)
 
-    shapes = tuple((pair(m), pair(m)) for m in (2 * GROUP * rows + 16, 2 * pad + 16))
-    pl.run_scoped(body, shapes)
+    m = 2 * GROUP * rows + 16
+    pl.run_scoped(body, (pair(m), pair(m)))
 
 
 def write_kernel(species, lam, out_ref, lam_out, sem):
@@ -459,7 +463,6 @@
     bins = lax.axis_size("bin")
     all_species, pts = table.shape
     rows = all_species // cols
-    pad = -(-rows // 8) * 8
     total_pts = pts * cols
     per_shard = slope.shape[0]
     sub = per_shard // cols // LANES
@@ -479,7 +482,7 @@
     dma = pltpu.SemaphoreType.DMA
     one = dma((1,))
     species, lam = pl.pallas_call(
-        functools.partial(scoped_kernel, cols, bins, total_pts, rows, pad),
+        functools.partial(scoped_kernel, cols, bins, total_pts, rows),
         out_shape=(
             jax.ShapeDtypeStruct((bins, cols, rows, width), jnp.float32),
             jax.ShapeDtypeStruct((bins, cols, sub, LANES), jnp.float32),
@@ -493,9 +496,8 @@
             pltpu.VMEM(packed, jnp.float32),
             pltpu.VMEM((cols, *packed[1:]), jnp.float32),
             pltpu.VMEM((2 * GROUP * rows + 16, total_pts), jnp.bfloat16),
-            pltpu.VMEM((2 * pad + 16, total_pts), jnp.bfloat16),
             pltpu.VMEM((2, STRIDE, 2 * LANES), jnp.float32),
-            pltpu.VMEM((items, GROUP, rows, width // PARTS), jnp.float32),
+            pltpu.VMEM((items + 1, GROUP, rows, width // PARTS), jnp.float32),
             dma((5,)), pltpu.SemaphoreType.REGULAR,
             one, one, one, one, one, dma((chips, groups)),
             one, dma((groups, GROUP)),

time: 33.1 us -> 32.4 us (0.979)
  Pallas kernels: 32.3 us -> 31.6 us
    pallas_call x1, Pallas kernels: 30.1 us -> 29.4 us  [per_device(): pl.pallas_call(functools.partial(scoped_kernel, cols, bins, total_pts, ro...]
where the time goes in v3:
time: 32.4 us; the launch traced here: 32.2 us
  Pallas kernels  31.6 us (98%)
  between operations  0.64 us (2%)
    pallas_call x1, Pallas kernels, per_device(): pl.pallas_call(functools.partial(scoped_kernel, cols, bins, total_pts, ro...  29.4 us
    pallas_call x1, Pallas kernels, per_device(): pl.pallas_call(write_kernel, out_shape=(jax.ShapeDtypeStruct((rows, per_s...  2.18 us

profile of v3, /device:TPU:0, one launch (start us, length us, event | category | flops | bytes accessed | tf_op | source)
XLA Modules:
  0.0 32.2 jit_solution(5335966682579563423)
XLA Ops:
  0.6 29.4 %shard_map.68 = (f32[4,8,8,4096]{3,2,1,0:T(8,128)S(1)}, f32[4,8,32,128]{3,2,1,0:T(8,128)S(1)}) custom-call(f32[8,32,128]{2,1,0:T(8,128)} %bitcast.6, f32[8,32,128]{2,1,0:T(8,128)} %bitcast.7, f32[8,32,128]{2,1,0:T(8,128)} %bitcast.8, f32[8,32,128]{2,1,0:T(8,128)} %bitcast.9, f32[8,8,64]{2,1,0:T(8,128)} %bitcast.10), custom_call_target="tpu_custom_call" | custom-call | tf_op jit(solution)/shard_map/pallas_call | solution.py:484
  30.0 2.2 %shard_map.69 = (f32[8,131072]{1,0:T(8,128)}, f32[4,8,32,128]{3,2,1,0:T(8,128)}) custom-call(f32[4,8,8,4096]{3,2,1,0:T(8,128)S(1)} %get-tuple-element.6.species, f32[4,8,32,128]{3,2,1,0:T(8,128)S(1)} %get-tuple-element.7.lam), custom_call_target="tpu_custom_call" | custom-call | tf_op jit(solution)/shard_map/pallas_call | solution.py:512

commit v4 on v3

--- a/solution.py
+++ b/solution.py
@@ -15,6 +15,7 @@
 STRIDE = 32
 DEPTH = 256
 GROUP = 4
+RANK = 2
 PARTS = 4
 SINGLE = 2
 
@@ -66,21 +67,28 @@
         pl.semaphore_signal(sem, inc=1, device_id=(c, b), device_id_type=MESH)
 
     barrier = pltpu.get_barrier_semaphore()
-    greet(barrier, col, partner)
-    for d in range(1, GROUP):
-        greet(barrier, peer(0, d), me)
-    for i in range(1, chips):
-        greet(barrier, col, other_chip(i))
-
-    def greet_group(sem, g):
-        for d in range(GROUP):
-            greet(sem, g * GROUP + d, me)
+    rank = col // RANK
+    ranks = cols // RANK
+
+    def greet_rank(sem, k):
+        for d in range(RANK):
+            greet(sem, k * RANK + d, me)
+
+    def greet_chips(sem, g):
         for i in range(1, chips):
             greet(sem, g * GROUP + member, other_chip(i))
 
-    @pl.loop(group + 1, groups)
+    greet(barrier, col, partner)
+    for d in range(1, RANK):
+        greet(barrier, rank * RANK + lax.rem(col + d, RANK), me)
+
+    @pl.loop(group, groups)
     def _(g):
-        greet_group(barrier, g)
+        greet_chips(barrier, g)
+
+    @pl.loop(rank + 1, ranks)
+    def _(k):
+        greet_rank(barrier, k)
 
     load_table = pltpu.make_async_copy(placed_hbm, placed, isem.at[4])
     load_table.start()
@@ -96,7 +104,6 @@
         for acc in pair:
             pltpu.matmul_pop(acc)
 
-    each = GROUP + chips - 1
     h = 1.0 / total_pts
     wide = STRIDE * h
     first = (lax.broadcasted_iota(jnp.int32, consts.shape[1:], 0).astype(jnp.float32) + 0.5) * h
@@ -116,29 +123,33 @@
         return remote(at, at, ksend.at[0], krecv.at[0], col, other_chip(i))
 
     def enter():
-        pl.semaphore_wait(barrier, (group + 1) * each)
+        pl.semaphore_wait(barrier, (rank + 1) * RANK + (group + 1) * (chips - 1))
+
+        @pl.loop(0, rank)
+        def _(k):
+            greet_rank(far, k)
 
         @pl.loop(0, group)
         def _(g):
-            greet_group(far, g)
-
-        @pl.loop(0, group)
-        def _(g):
-            for d in range(GROUP):
-                table_copy(g * GROUP + d).start()
-
-        for d in range(1, GROUP):
-            table_copy(peer(0, d)).start()
+            greet_chips(far, g)
+
+        @pl.loop(0, rank)
+        def _(k):
+            for d in range(RANK):
+                table_copy(k * RANK + d).start()
+
+        for d in range(1, RANK):
+            table_copy(rank * RANK + lax.rem(col + d, RANK)).start()
         tab[col] = packed[group]
+        for i in range(1, chips):
+            curve_copy(i).start()
 
     for load in loads:
         load.wait()
 
-    @pl.when(group == last)
+    @pl.when(rank > 0)
     def _():
         enter()
-        for i in range(1, chips):
-            curve_copy(i).start()
 
     curve2 = curve[me, col] * LOG2E
     target = own[1]
@@ -172,7 +183,7 @@
 
     lam_ref[me, col] = lax.fori_loop(0, ITERS, lambda _, lam: newton(lam), own[0])
 
-    @pl.when(group < last)
+    @pl.when(rank == 0)
     def _():
         enter()
 
@@ -195,19 +206,17 @@
 
     for i in range(1, chips):
         first_copy(i, 0).start()
+    @pl.when(rank < ranks - 1)
+    def _():
+        pl.semaphore_wait(far, (ranks - 1 - rank) * RANK + (last - group) * (chips - 1))
+
+        @pl.loop(rank + 1, ranks)
+        def _(k):
+            for d in range(RANK):
+                table_copy(k * RANK + d).start()
+
     for d in range(1, GROUP):
         second_copy(0, 0, d).start()
-
-    @pl.when(group < last)
-    def _():
-        for i in range(1, chips):
-            curve_copy(i).start()
-        pl.semaphore_wait(far, (last - group) * each)
-
-        @pl.loop(group + 1, groups)
-        def _(g):
-            for d in range(GROUP):
-                table_copy(g * GROUP + d).start()
 
     @pl.loop(1, groups)
     def _(u):
@@ -243,7 +252,7 @@
             for m in range(steps):
                 e_hi = e.astype(jnp.bfloat16)
                 highs.append(e_hi)
-                lows.append((e - e_hi.astype(jnp.float32)).astype(jnp.bfloat16))
+                lows.append(e - e_hi.astype(jnp.float32))
                 if n < tiles - 1 or m < steps - 1:
                     e = e * ratio
                     ratio = ratio * turn
@@ -277,7 +286,9 @@
     def y_arrivals(u, k):
         for i in range(1, chips):
             total_of(species.at[0, pl.ds(0, GROUP), :, pl.ds(0, part)], ysend.at[0], yrecv.at[i - 1, u, k]).wait_recv()
-            for d in range(GROUP):
+
+            @pl.loop(0, GROUP)
+            def _(d):
                 hand_on(other_chip(i), peer(u, d), PARTS - SINGLE + k)
 
     count = SINGLE + chips
@@ -326,7 +337,8 @@
 
         @pl.when(item < spare)
         def _():
-            for d in range(1, GROUP):
+            @pl.loop(1, GROUP)
+            def _(d):
                 member_copy(item, d, b, j, q).start()
 
         @pl.when(single)
@@ -338,14 +350,18 @@
 
     def single_arrivals(u, k):
         member_arrivals(u * per + k)
-        for d in range(1, GROUP):
+
+        @pl.loop(1, GROUP)
+        def _(d):
             for i in range(1, chips):
                 y_copy(i, u, d, k).start()
             hand_on(me, peer(u, d), PARTS - SINGLE + k)
 
     def double_arrivals(u, i):
         member_arrivals(u * per + SINGLE + i)
-        for d in range(1, GROUP):
+
+        @pl.loop(1, GROUP)
+        def _(d):
             hand_on(other_chip(i), peer(u, d), 1)
 
     def ready(n):
@@ -449,9 +465,12 @@
 
 def write_kernel(species, lam, out_ref, lam_out, sem):
     bins, cols, _, width = species.shape
-    for b in range(bins):
+    @pl.loop(0, bins)
+    def _(b):
         for j in range(cols):
-            pltpu.make_async_copy(species.at[b, j], out_ref.at[:, pl.ds((b * cols + j) * width, width)], sem.at[0]).start()
+            to = pl.ds(pl.multiple_of((b * cols + j) * width, LANES), width)
+            pltpu.make_async_copy(species.at[b, j], out_ref.at[:, to], sem.at[0]).start()
+
     keep = pltpu.make_async_copy(lam, lam_out, sem.at[1])
     keep.start()
     pltpu.make_async_copy(out_ref, out_ref, sem.at[0]).wait()

time: 32.4 us -> 31.6 us (0.975)
  Pallas kernels: 31.6 us -> 30.8 us
    pallas_call x1, Pallas kernels: 29.4 us -> 28.7 us  [per_device(): pl.pallas_call(functools.partial(scoped_kernel, cols, bins, total_pts, ro...]
where the time goes in v4:
time: 31.6 us; the launch traced here: 31.5 us
  Pallas kernels  30.8 us (97%)
  between operations  0.64 us (2%)
    pallas_call x1, Pallas kernels, per_device(): pl.pallas_call(functools.partial(scoped_kernel, cols, bins, total_pts, ro...  28.7 us
    pallas_call x1, Pallas kernels, per_device(): pl.pallas_call(write_kernel, out_shape=(jax.ShapeDtypeStruct((rows, per_s...  2.18 us

profile of v4, /device:TPU:0, one launch (start us, length us, event | category | flops | bytes accessed | tf_op | source)
XLA Modules:
  0.0 31.5 jit_solution(7144528596241562717)
XLA Ops:
  0.6 28.7 %shard_map.68 = (f32[4,8,8,4096]{3,2,1,0:T(8,128)S(1)}, f32[4,8,32,128]{3,2,1,0:T(8,128)S(1)}) custom-call(f32[8,32,128]{2,1,0:T(8,128)} %bitcast.6, f32[8,32,128]{2,1,0:T(8,128)} %bitcast.7, f32[8,32,128]{2,1,0:T(8,128)} %bitcast.8, f32[8,32,128]{2,1,0:T(8,128)} %bitcast.9, f32[8,8,64]{2,1,0:T(8,128)} %bitcast.10), custom_call_target="tpu_custom_call" | custom-call | tf_op jit(solution)/shard_map/pallas_call | solution.py:503
  29.3 2.2 %shard_map.69 = (f32[8,131072]{1,0:T(8,128)}, f32[4,8,32,128]{3,2,1,0:T(8,128)}) custom-call(f32[4,8,8,4096]{3,2,1,0:T(8,128)S(1)} %get-tuple-element.6.species, f32[4,8,32,128]{3,2,1,0:T(8,128)S(1)} %get-tuple-element.7.lam), custom_call_target="tpu_custom_call" | custom-call | tf_op jit(solution)/shard_map/pallas_call | solution.py:531

commit v5 on v4

--- a/solution.py
+++ b/solution.py
@@ -337,8 +337,7 @@
 
         @pl.when(item < spare)
         def _():
-            @pl.loop(1, GROUP)
-            def _(d):
+            for d in range(1, GROUP):
                 member_copy(item, d, b, j, q).start()
 
         @pl.when(single)
@@ -375,7 +374,7 @@
                 for d in range(1, GROUP):
                     second_copy(u, 0, d).start()
 
-            @pl.when(r == SINGLE + 1)
+            @pl.when(r == SINGLE)
             def _():
                 for i in range(1, chips):
                     first_arrival(i, u).wait_recv()
@@ -386,16 +385,23 @@
                 def _():
                     total_of(curve.at[pl.ds(0, chips - 1), :, pl.ds(0, 2 * part_rows)], ksend.at[0], krecv.at[0]).wait_recv()
 
-        m = n - locals_from
-
-        @pl.when(jnp.logical_and(m >= 0, lax.rem(m, chips) == 0))
-        def _():
-            second_arrival(m // others, 1 + lax.rem(m, others) // chips).wait_recv()
-
+    def spread_two(e):
+        for x in range(2):
+            k = 2 * e + x
+            second_arrival(k // (GROUP - 1), 1 + lax.rem(k, GROUP - 1)).wait_recv()
+
+    def hand_on_lam(_):
+        for i in range(chips):
+            at = lam_ref.at[other_chip(i)]
+            remote(at, at, lsend.at[0], lrecv.at[0], col, partner).start()
+
+    doubles_pair, locals_pair, pairs = doubles_from // 2, locals_from // 2, total // 2
     events = (
-        (doubles_from, 2, groups * SINGLE, lambda e: single_arrivals(e // SINGLE, lax.rem(e, SINGLE))),
-        (locals_from + 4, 3, groups * SINGLE, lambda e: y_arrivals(e // SINGLE, lax.rem(e, SINGLE))),
-        (locals_from + 5, 2, groups * chips, lambda e: double_arrivals(e // chips, lax.rem(e, chips))),
+        (doubles_pair + 1, 2, groups * (GROUP - 1) // 2, spread_two),
+        (pairs - 2, 1, 1, hand_on_lam),
+        *((doubles_pair + k, 3, groups, lambda u, k=k: single_arrivals(u, k)) for k in range(SINGLE)),
+        (locals_pair + 3, 2, groups * SINGLE, lambda e: y_arrivals(e // SINGLE, lax.rem(e, SINGLE))),
+        (locals_pair + 4, 1, groups * chips, lambda e: double_arrivals(e // chips, lax.rem(e, chips))),
     )
 
     def served(n):
@@ -406,38 +412,38 @@
             def _():
                 event(m // every)
 
-    @pl.loop(0, total)
-    def _(n):
-        ready(n)
-        back = jnp.maximum(n - 1, 0)
-        for t in range(blocks):
-            start(n, t)
-            if t > 0:
-                done(n, t - 1)
-            elif lag:
-                done(back, blocks - 1)
-                keep(back)
-        if lag:
-            @pl.when(n > 0)
-            def _():
-                sent(back)
-        else:
-            done(n, blocks - 1)
-            keep(n)
-            sent(n)
-        served(n)
+    @pl.loop(0, pairs)
+    def _(p):
+        ready(2 * p)
+        for x in range(2):
+            n = 2 * p + x
+            back = n - 1 if x else jnp.maximum(n - 1, 0)
+            for t in range(blocks):
+                start(n, t)
+                if t > 0:
+                    done(n, t - 1)
+                elif lag:
+                    done(back, blocks - 1)
+                    keep(back)
+                    if x:
+                        sent(back)
+                    else:
+                        @pl.when(p > 0)
+                        def _():
+                            sent(back)
+            if not lag:
+                done(n, blocks - 1)
+                keep(n)
+                sent(n)
+        served(p)
 
     if lag:
         done(total - 1, blocks - 1)
         keep(total - 1)
         sent(total - 1)
 
-    for i in range(chips):
-        at = lam_ref.at[other_chip(i)]
-        remote(at, at, lsend.at[0], lrecv.at[0], col, partner).start()
-
     for begin, every, number, event in reversed(events):
-        @pl.loop(max(0, min(number, -((begin - total) // every))), number)
+        @pl.loop(max(0, min(number, -((begin - pairs) // every))), number)
         def _(e):
             event(e)
 

time: 31.6 us -> 30 us (0.949)
  Pallas kernels: 30.8 us -> 29.2 us
    pallas_call x1, Pallas kernels: 28.7 us -> 27 us  [per_device(): pl.pallas_call(functools.partial(scoped_kernel, cols, bins, total_pts, ro...]
where the time goes in v5:
time: 30 us; the launch traced here: 29.9 us
  Pallas kernels  29.2 us (97%)
  between operations  0.64 us (2%)
    pallas_call x1, Pallas kernels, per_device(): pl.pallas_call(functools.partial(scoped_kernel, cols, bins, total_pts, ro...  27 us
    pallas_call x1, Pallas kernels, per_device(): pl.pallas_call(write_kernel, out_shape=(jax.ShapeDtypeStruct((rows, per_s...  2.18 us

profile of v5, /device:TPU:0, one launch (start us, length us, event | category | flops | bytes accessed | tf_op | source)
XLA Modules:
  0.0 29.9 jit_solution(15137716020800637508)
XLA Ops:
  0.6 27.0 %shard_map.68 = (f32[4,8,8,4096]{3,2,1,0:T(8,128)S(1)}, f32[4,8,32,128]{3,2,1,0:T(8,128)S(1)}) custom-call(f32[8,32,128]{2,1,0:T(8,128)} %bitcast.6, f32[8,32,128]{2,1,0:T(8,128)} %bitcast.7, f32[8,32,128]{2,1,0:T(8,128)} %bitcast.8, f32[8,32,128]{2,1,0:T(8,128)} %bitcast.9, f32[8,8,64]{2,1,0:T(8,128)} %bitcast.10), custom_call_target="tpu_custom_call" | custom-call | tf_op jit(solution)/shard_map/pallas_call | solution.py:509
  27.7 2.2 %shard_map.69 = (f32[8,131072]{1,0:T(8,128)}, f32[4,8,32,128]{3,2,1,0:T(8,128)}) custom-call(f32[4,8,8,4096]{3,2,1,0:T(8,128)S(1)} %get-tuple-element.6.species, f32[4,8,32,128]{3,2,1,0:T(8,128)S(1)} %get-tuple-element.7.lam), custom_call_target="tpu_custom_call" | custom-call | tf_op jit(solution)/shard_map/pallas_call | solution.py:537

commit v6 on v5

--- a/solution.py
+++ b/solution.py
@@ -399,7 +399,7 @@
     events = (
         (doubles_pair + 1, 2, groups * (GROUP - 1) // 2, spread_two),
         (pairs - 2, 1, 1, hand_on_lam),
-        *((doubles_pair + k, 3, groups, lambda u, k=k: single_arrivals(u, k)) for k in range(SINGLE)),
+        *((doubles_pair + 2 * k, 3, groups, lambda u, k=k: single_arrivals(u, k)) for k in range(SINGLE)),
         (locals_pair + 3, 2, groups * SINGLE, lambda e: y_arrivals(e // SINGLE, lax.rem(e, SINGLE))),
         (locals_pair + 4, 1, groups * chips, lambda e: double_arrivals(e // chips, lax.rem(e, chips))),
     )

time: 30 us -> 30.1 us (level)
  no operation moved by 1% of the time
where the time goes in v6:
time: 30.1 us; the launch traced here: 29.9 us
  Pallas kernels  29.2 us (97%)
  between operations  0.64 us (2%)
    pallas_call x1, Pallas kernels, per_device(): pl.pallas_call(functools.partial(scoped_kernel, cols, bins, total_pts, ro...  27 us
    pallas_call x1, Pallas kernels, per_device(): pl.pallas_call(write_kernel, out_shape=(jax.ShapeDtypeStruct((rows, per_s...  2.18 us

profile of v6, /device:TPU:0, one launch (start us, length us, event | category | flops | bytes accessed | tf_op | source)
XLA Modules:
  0.0 29.9 jit_solution(13815559098706641260)
XLA Ops:
  0.6 27.0 %shard_map.68 = (f32[4,8,8,4096]{3,2,1,0:T(8,128)S(1)}, f32[4,8,32,128]{3,2,1,0:T(8,128)S(1)}) custom-call(f32[8,32,128]{2,1,0:T(8,128)} %bitcast.6, f32[8,32,128]{2,1,0:T(8,128)} %bitcast.7, f32[8,32,128]{2,1,0:T(8,128)} %bitcast.8, f32[8,32,128]{2,1,0:T(8,128)} %bitcast.9, f32[8,8,64]{2,1,0:T(8,128)} %bitcast.10), custom_call_target="tpu_custom_call" | custom-call | tf_op jit(solution)/shard_map/pallas_call | solution.py:509
  27.7 2.2 %shard_map.69 = (f32[8,131072]{1,0:T(8,128)}, f32[4,8,32,128]{3,2,1,0:T(8,128)}) custom-call(f32[4,8,8,4096]{3,2,1,0:T(8,128)S(1)} %get-tuple-element.6.species, f32[4,8,32,128]{3,2,1,0:T(8,128)S(1)} %get-tuple-element.7.lam), custom_call_target="tpu_custom_call" | custom-call | tf_op jit(solution)/shard_map/pallas_call | solution.py:537
